TPU v7x, 32 devices: a whole 2x2x4 slice. The times are simulated.
32 devices in a mesh: node: 4 (over y, core), rep: 8 (over z, x).
Axes of the slice: x: 2, y: 2, z: 4, core: 2. Of those that a mesh axis runs over, the one named last changes fastest.
Arguments:
- tokens: bfloat16 [8192, 2048], P(('node', 'rep')), may hold values from -60 to 60
- cotangent: bfloat16 [8192, 512], P(('node', 'rep')), may hold values from -6 to 6
- value_weight: bfloat16 [2048, 512], P('node'), may hold values from -0.25 to 0.25
Outputs:
- input_grad: bfloat16 [8192, 2048], P(('node', 'rep'))
- update: float32 [2048, 512], P('node')
All inputs are finite; a program needn't handle non-finite values.
Results may differ from a plain program's by a relative error of at most 0.025.
Values may be sent and summed in bfloat16 or wider, within the bound.
A program may use at most 64 MiB of HBM per device.

v0:
```python
import math
import jax
import jax.numpy as jnp
from jax import lax
from jax.sharding import PartitionSpec as P

DIN = 2048
HD = 128
NS_ITERS = 5
coef_a = 3.4445
coef_b = -4.775
coef_c = 2.0315
epsilon = 1e-07


def per_device(tokens, cotangent, value_weight):
    width = value_weight.shape[1]
    local_rows = value_weight.shape[0]
    heads = width // HD
    input_grad = lax.dot_general(
        cotangent,
        lax.all_gather(value_weight, "node", axis=0, tiled=True),
        (((1,), (1,)), ((), ())),
        preferred_element_type=jnp.float32,
    ).astype(jnp.bfloat16)
    partial_rows = lax.psum_scatter(
        lax.dot_general(
            tokens, cotangent, (((0,), (0,)), ((), ())), preferred_element_type=jnp.float32
        ).astype(jnp.bfloat16),
        "node",
        scatter_dimension=0,
        tiled=True,
    ).astype(jnp.float32)
    gradient = lax.psum(partial_rows, "rep")
    blocks = gradient.reshape(local_rows, heads, HD)
    local_raw = jnp.einsum("rhi,rhj->hij", blocks, blocks, precision=lax.Precision.HIGHEST)
    gram_raw = lax.psum(local_raw, "node")
    squares = jnp.einsum("hii->h", gram_raw)
    divisor = jnp.sqrt(squares) + epsilon
    start_iterate = blocks / divisor[None, :, None]
    gram = gram_raw / (divisor * divisor)[:, None, None]
    identity = jnp.broadcast_to(jnp.eye(HD, dtype=jnp.float32), (heads, HD, HD))
    total = identity
    for step in range(NS_ITERS):
        factor = (
            coef_a * identity
            + coef_b * gram
            + coef_c * jnp.einsum("hij,hjk->hik", gram, gram, precision=lax.Precision.HIGHEST)
        )
        total = jnp.einsum("hij,hjk->hik", total, factor, precision=lax.Precision.HIGHEST)
        if step + 1 < NS_ITERS:
            halfway = jnp.einsum("hij,hjk->hik", gram, factor, precision=lax.Precision.HIGHEST)
            gram = jnp.einsum("hji,hjk->hik", factor, halfway, precision=lax.Precision.HIGHEST)
    iterate = jnp.einsum("rhi,hij->rhj", start_iterate, total, precision=lax.Precision.HIGHEST)
    update = 0.2 * math.sqrt(DIN) * iterate.reshape(local_rows, width)
    return (input_grad, update)


def solution(mesh):
    in_specs = (P(("node", "rep"), None), P(("node", "rep"), None), P("node", None))
    out_specs = (P(("node", "rep"), None), P("node", None))
    return jax.shard_map(
        per_device, mesh=mesh, in_specs=in_specs, out_specs=out_specs, check_vma=False
    )
```

profile of v0, /device:TPU:0, one launch (start us, length us, event | category | flops | bytes accessed | tf_op | source)
XLA Modules:
  0.0 206.4 jit_solution(13655678280055105823)
XLA Ops:
  7.2 0.0 copy-start
  7.2 0.0 reduce-scatter.2.cloned.1.call-start
  7.2 1.2 copy-done
  8.4 3.0 %convolution_convert_fusion = bf16[2048,512]{1,0:T(8,128)(2,1)} fusion(bf16[256,2048]{1,0:T(8,128)(2,1)S(1)} %copy-done, bf16[256,512]{1,0:T(8,128)(2,1)} %param.4), kind=kOutput, calls=%fused_computation | convolution fusion | flops 537919488 | bytes 3407872 | tf_op jit(solution)/shard_map/dot_general | solution.py:27
  11.4 0.0 reduce-scatter.2.cloned.1.call-update
  11.5 0.0 all-reduce.3.cloned.1.call-start
  11.5 34.0 %reduce-scatter.2.cloned.1.call-done = bf16[512,512]{1,0:T(8,128)(2,1)} async-done(((bf16[2048,512]{1,0:T(8,128)(2,1)}), bf16[512,512]{1,0:T(8,128)(2,1)}) %reduce-scatter.2.cloned.1.call-update) | async-done | bytes 524304 | tf_op jit(solution)/shard_map/reduce_scatter | solution.py:26
  45.5 2.1 %copy_bitcast_fusion = f32[512,4,128]{2,0,1:T(8,128)} fusion(bf16[512,512]{1,0:T(8,128)(2,1)} %reduce-scatter.2.cloned.1.call-done), kind=kLoop, calls=%fused_computation.13 | loop fusion | flops 262144 | bytes 1572864 | tf_op jit(solution)/shard_map/reshape | solution.py:35
  47.6 0.0 copy-start.2
  47.6 0.0 all-reduce.3.cloned.1.call-update
  47.6 0.0 all-gather.2.cloned.1.call-start
  47.7 0.7 all-gather.2.cloned.1.call-update
  48.4 0.0 all-reduce.5.cloned.1.call-start
  48.5 79.5 %all-reduce.3.cloned.1.call-done = f32[512,4,128]{2,0,1:T(8,128)} async-done(((f32[512,4,128]{2,0,1:T(8,128)}), f32[512,4,128]{2,0,1:T(8,128)}) %all-reduce.3.cloned.1.call-update) | async-done | bytes 1048592 | tf_op jit(solution)/shard_map/psum | solution.py:34
  128.0 4.1 %fusion.13 = f32[4,128,128]{2,1,0:T(8,128)} fusion(f32[512,4,128]{2,0,1:T(8,128)} %all-reduce.3.cloned.1.call-done), kind=kOutput, calls=%fused_computation.28 | convolution fusion | flops 402653184 | bytes 1310720 | tf_op jit(solution)/shard_map/rhi,rhj->hij/dot_general | solution.py:36
  132.1 0.0 all-reduce.5.cloned.1.call-update
  132.1 19.6 %all-gather.2.cloned.1.call-done = bf16[2048,512]{1,0:T(8,128)(2,1)} async-done(((bf16[512,512]{1,0:T(8,128)(2,1)}), bf16[2048,512]{1,0:T(8,128)(2,1)}) %all-gather.2.cloned.1.call-update) | async-done | bytes 2097168 | tf_op jit(solution)/shard_map/all_gather | solution.py:22
  151.8 0.0 copy-done.2
  151.8 3.3 %convolution_convert_fusion.1 = bf16[256,2048]{1,0:T(8,128)(2,1)} fusion(bf16[256,512]{1,0:T(8,128)(2,1)S(1)} %copy-done.2, bf16[2048,512]{1,0:T(8,128)(2,1)} %all-gather.2.cloned.1.call-done), kind=kOutput, calls=%fused_computation.1 | convolution fusion | flops 537395200 | bytes 3407872 | tf_op jit(solution)/shard_map/dot_general | solution.py:20
  155.1 31.8 %all-reduce.5.cloned.1.call-done = f32[4,128,128]{2,1,0:T(8,128)} async-done(((f32[4,128,128]{2,1,0:T(8,128)}), f32[4,128,128]{2,1,0:T(8,128)}) %all-reduce.5.cloned.1.call-update) | async-done | bytes 262160 | tf_op jit(solution)/shard_map/psum | solution.py:37
  186.8 0.0 copy-start.3
  186.8 1.2 select_reduce_fusion
  188.0 1.6 fusion.4
  189.6 0.4 fusion.7
  190.0 0.0 copy-done.3
  190.0 0.4 fusion.11
  190.5 0.6 fusion.14
  191.1 0.4 fusion.3
  191.4 0.4 fusion.16
  191.8 0.4 fusion.15
  192.2 0.6 fusion.17
  192.9 0.4 fusion.2
  193.2 0.4 fusion.19
  193.6 0.4 fusion.18
  194.0 0.6 fusion.20
  194.7 0.4 fusion.1
  195.0 0.0 copy-start.1
  195.0 0.4 fusion.22
  195.4 0.4 fusion.21
  195.9 0.6 fusion.23
  196.5 0.4 fusion
  196.8 0.6 fusion.24
  197.4 0.0 copy-done.1
  197.5 1.1 convolution_multiply_fusion
  198.5 1.3 copy.11
  (4 shorter events, 0.0 us)
Async XLA Ops:
  7.2 1.2 copy-start
  7.2 38.4 %reduce-scatter.2.cloned.1.call-start = ((), (), s32[]{:S(2)}) async-start(), calls=%async_computation.2 | async-start | bytes 2621440 | tf_op jit(solution)/shard_map/reduce_scatter | solution.py:26
  11.5 116.6 %all-reduce.3.cloned.1.call-start = ((), (), s32[]{:S(2)}) async-start(), calls=%async_computation.3 | async-start | bytes 2097152 | tf_op jit(solution)/shard_map/psum | solution.py:34
  47.6 104.2 %copy-start.2 = (bf16[256,512]{1,0:T(8,128)(2,1)S(1)}, bf16[256,512]{1,0:T(8,128)(2,1)}, u32[]{:S(2)}) copy-start(bf16[256,512]{1,0:T(8,128)(2,1)} %param.4) | copy-start | bytes 786436
  47.6 104.1 %all-gather.2.cloned.1.call-start = ((), (), s32[]{:S(2)}) async-start(), calls=%async_computation.1 | async-start | bytes 2621440 | tf_op jit(solution)/shard_map/all_gather | solution.py:22
  48.4 138.5 %all-reduce.5.cloned.1.call-start = ((), (), s32[]{:S(2)}) async-start(), calls=%async_computation.4 | async-start | bytes 524288 | tf_op jit(solution)/shard_map/psum | solution.py:37
  186.8 3.2 %copy-start.3 = (f32[4,128,128]{2,1,0:T(8,128)S(1)}, f32[4,128,128]{2,1,0:T(8,128)}, u32[]{:S(2)}) copy-start(f32[4,128,128]{2,1,0:T(8,128)} %all-reduce.5.cloned.1.call-done) | copy-start | bytes 786436
  195.0 2.4 %copy-start.1 = (f32[512,4,128]{2,0,1:T(8,128)S(1)}, f32[512,4,128]{2,0,1:T(8,128)}, u32[]{:S(2)}) copy-start(f32[512,4,128]{2,0,1:T(8,128)} %all-reduce.3.cloned.1.call-done) | copy-start | bytes 3145732
Sparse Core Ops, SparseCore 0:
  11.6 33.9 reduce-scatter.1
  49.6 78.3 all-reduce.2
  129.6 22.1 all-gather.1
  154.5 32.2 all-reduce.4
where the time goes:
time: 207 us; the launch traced here: 206 us
  waiting for transfers between devices  166 us (80%)
  matrix products  20.8 us (10%)
  between operations  14 us (7%)
  other arithmetic  3.28 us (2%)
  local copies, waits for them, and re-layouts  2.5 us (1%)
    psum x1, waiting for transfers between devices, per_device(): gradient = lax.psum(partial_rows, 'rep')  79.5 us
    reduce_scatter x1, waiting for transfers between devices, per_device(): lax.psum_scatter(lax.dot_general(tokens, cotangent, (((0,), (0,)), ((), (...  34 us
    psum x1, waiting for transfers between devices, per_device(): gram_raw = lax.psum(local_raw, 'node')  31.8 us
    all_gather x1, waiting for transfers between devices, per_device(): lax.all_gather(value_weight, 'node', axis=0, tiled=True)  19.6 us
  transfers between devices with their start and end apart: 4, of which 4 were waited for; matrix products, arithmetic and copies ran while one was open for 4% of the time, Pallas kernels for 0%

commit v1 on v0

--- a/solution.py
+++ b/solution.py
@@ -34,7 +34,9 @@
     gradient = lax.psum(partial_rows, "rep")
     blocks = gradient.reshape(local_rows, heads, HD)
     local_raw = jnp.einsum("rhi,rhj->hij", blocks, blocks, precision=lax.Precision.HIGHEST)
-    gram_raw = lax.psum(local_raw, "node")
+    gram_raw = local_raw
+    for hop in (1, 2):
+        gram_raw = gram_raw + lax.ppermute(gram_raw, "node", [(dev, dev ^ hop) for dev in range(4)])
     squares = jnp.einsum("hii->h", gram_raw)
     divisor = jnp.sqrt(squares) + epsilon
     start_iterate = blocks / divisor[None, :, None]

time: 207 us -> 175 us (0.85)
  waiting for transfers between devices: 166 us -> 135 us
    psum x1 -> x0, waiting for transfers between devices: 31.8 us -> none  [per_device(): gram_raw = lax.psum(local_raw, 'node')]
  transfers between devices with their start and end apart: 4 -> 5, of which waited for: 4 -> 4; matrix products, arithmetic and copies ran while one was open for 4% -> 4% of each run, Pallas kernels for 0% -> 0%
where the time goes in v1:
time: 175 us
  waiting for transfers between devices  135 us (77%)
  matrix products  18.9 us (11%)
  between operations  14 us (8%)
  local copies, waits for them, and re-layouts  2.49 us (1%)
  other arithmetic  2.3 us (1%)
    psum x1, waiting for transfers between devices, per_device(): gradient = lax.psum(partial_rows, 'rep')  79.6 us
    reduce_scatter x1, waiting for transfers between devices, per_device(): lax.psum_scatter(lax.dot_general(tokens, cotangent, (((0,), (0,)), ((), (...  34 us
    all_gather x1, waiting for transfers between devices, per_device(): lax.all_gather(value_weight, 'node', axis=0, tiled=True)  19.6 us
  transfers between devices with their start and end apart: 5, of which 4 were waited for; matrix products, arithmetic and copies ran while one was open for 4% of the time, Pallas kernels for 0%

profile of v1, /device:TPU:0, one launch (start us, length us, event | category | flops | bytes accessed | tf_op | source)
XLA Modules:
  0.0 174.9 jit_solution(6550995823562379731)
XLA Ops:
  7.2 0.0 copy-start
  7.2 0.0 reduce-scatter.2.cloned.1.call-start
  7.2 1.2 copy-done
  8.4 3.0 %convolution_convert_fusion = bf16[2048,512]{1,0:T(8,128)(2,1)} fusion(bf16[256,2048]{1,0:T(8,128)(2,1)S(1)} %copy-done, bf16[256,512]{1,0:T(8,128)(2,1)} %param.4), kind=kOutput, calls=%fused_computation | convolution fusion | flops 537919488 | bytes 3407872 | tf_op jit(solution)/shard_map/dot_general | solution.py:27
  11.4 0.0 reduce-scatter.2.cloned.1.call-update
  11.5 0.0 all-reduce.2.cloned.1.call-start
  11.5 34.0 %reduce-scatter.2.cloned.1.call-done = bf16[512,512]{1,0:T(8,128)(2,1)} async-done(((bf16[2048,512]{1,0:T(8,128)(2,1)}), bf16[512,512]{1,0:T(8,128)(2,1)}) %reduce-scatter.2.cloned.1.call-update) | async-done | bytes 524304 | tf_op jit(solution)/shard_map/reduce_scatter | solution.py:26
  45.5 2.1 %copy_bitcast_fusion = f32[512,4,128]{2,0,1:T(8,128)} fusion(bf16[512,512]{1,0:T(8,128)(2,1)} %reduce-scatter.2.cloned.1.call-done), kind=kLoop, calls=%fused_computation.12 | loop fusion | flops 262144 | bytes 1572864 | tf_op jit(solution)/shard_map/reshape | solution.py:35
  47.6 0.0 all-reduce.2.cloned.1.call-update
  47.6 0.0 copy-start.2
  47.7 0.0 all-gather.2.cloned.1.call-start
  47.7 0.7 all-gather.2.cloned.1.call-update
  48.4 79.6 %all-reduce.2.cloned.1.call-done = f32[512,4,128]{2,0,1:T(8,128)} async-done(((f32[512,4,128]{2,0,1:T(8,128)}), f32[512,4,128]{2,0,1:T(8,128)}) %all-reduce.2.cloned.1.call-update) | async-done | bytes 1048592 | tf_op jit(solution)/shard_map/psum | solution.py:34
  128.0 3.4 %fusion.12 = f32[4,128,128]{2,1,0:T(8,128)S(1)} fusion(f32[512,4,128]{2,0,1:T(8,128)} %all-reduce.2.cloned.1.call-done), kind=kOutput, calls=%fused_computation.28 | convolution fusion | flops 402653184 | bytes 1310720 | tf_op jit(solution)/shard_map/rhi,rhj->hij/dot_general | solution.py:36
  131.4 0.1 collective-permute-start
  131.5 1.5 collective-permute-done
  133.0 1.5 collective-permute-start.1
  134.6 19.6 %all-gather.2.cloned.1.call-done = bf16[2048,512]{1,0:T(8,128)(2,1)} async-done(((bf16[512,512]{1,0:T(8,128)(2,1)}), bf16[2048,512]{1,0:T(8,128)(2,1)}) %all-gather.2.cloned.1.call-update) | async-done | bytes 2097168 | tf_op jit(solution)/shard_map/all_gather | solution.py:22
  154.2 0.0 copy-done.2
  154.2 3.3 %convolution_convert_fusion.1 = bf16[256,2048]{1,0:T(8,128)(2,1)} fusion(bf16[256,512]{1,0:T(8,128)(2,1)S(1)} %copy-done.2, bf16[2048,512]{1,0:T(8,128)(2,1)} %all-gather.2.cloned.1.call-done), kind=kOutput, calls=%fused_computation.1 | convolution fusion | flops 537395200 | bytes 3407872 | tf_op jit(solution)/shard_map/dot_general | solution.py:20
  157.5 0.0 collective-permute-done.1
  157.5 0.1 select_reduce_fusion
  157.7 0.5 add_add_fusion
  158.1 0.4 fusion.10
  158.6 0.4 fusion.6
  159.0 0.6 fusion.13
  159.6 0.4 fusion.3
  160.0 0.4 fusion.15
  160.4 0.4 fusion.14
  160.8 0.6 fusion.16
  161.4 0.4 fusion.2
  161.8 0.4 fusion.18
  162.2 0.4 fusion.17
  162.6 0.6 fusion.19
  163.2 0.4 fusion.1
  163.6 0.0 copy-start.1
  163.6 0.4 fusion.21
  164.0 0.4 fusion.20
  164.4 0.6 fusion.22
  165.0 0.4 fusion
  165.4 0.6 fusion.23
  166.0 0.0 copy-done.1
  166.0 1.1 convolution_multiply_fusion
  167.1 1.3 copy.11
  (5 shorter events, 0.1 us)
Async XLA Ops:
  7.2 1.2 copy-start
  7.2 38.4 %reduce-scatter.2.cloned.1.call-start = ((), (), s32[]{:S(2)}) async-start(), calls=%async_computation.2 | async-start | bytes 2621440 | tf_op jit(solution)/shard_map/reduce_scatter | solution.py:26
  11.5 116.6 %all-reduce.2.cloned.1.call-start = ((), (), s32[]{:S(2)}) async-start(), calls=%async_computation.3 | async-start | bytes 2097152 | tf_op jit(solution)/shard_map/psum | solution.py:34
  47.6 106.6 %copy-start.2 = (bf16[256,512]{1,0:T(8,128)(2,1)S(1)}, bf16[256,512]{1,0:T(8,128)(2,1)}, u32[]{:S(2)}) copy-start(bf16[256,512]{1,0:T(8,128)(2,1)} %param.4) | copy-start | bytes 786436
  47.7 106.5 %all-gather.2.cloned.1.call-start = ((), (), s32[]{:S(2)}) async-start(), calls=%async_computation.1 | async-start | bytes 2621440 | tf_op jit(solution)/shard_map/all_gather | solution.py:22
  131.4 1.6 collective-permute-start
  133.0 24.5 %collective-permute-start.1 = (f32[4,128,128]{2,1,0:T(8,128)S(1)}, f32[4,128,128]{2,1,0:T(8,128)S(1)}, u32[]{:S(2)}, u32[]{:S(2)}) collective-permute-start(f32[4,128,128]{2,1,0:T(8,128)S(1)} %add.51), channel_id=1, source_target_pairs={{0,16},{8,24},{16,0},{24,8},{1,17},{9,25},{17,1},{25,9},{2,18},{10... | collective-permute-start | bytes 786440 | tf_op jit(solution)/shard_map/ppermute | solution.py:39
  163.6 2.4 %copy-start.1 = (f32[512,4,128]{2,0,1:T(8,128)S(1)}, f32[512,4,128]{2,0,1:T(8,128)}, u32[]{:S(2)}) copy-start(f32[512,4,128]{2,0,1:T(8,128)} %all-reduce.2.cloned.1.call-done) | copy-start | bytes 3145732
Sparse Core Ops, SparseCore 0:
  11.6 33.9 reduce-scatter.1
  49.6 78.3 all-reduce.1
  129.6 24.5 all-gather.1

commit v2 on v0

--- a/solution.py
+++ b/solution.py
@@ -31,7 +31,9 @@
         scatter_dimension=0,
         tiled=True,
     ).astype(jnp.float32)
-    gradient = lax.psum(partial_rows, "rep")
+    gradient = partial_rows
+    for hop in (1, 2, 4):
+        gradient = gradient + lax.ppermute(gradient, "rep", [(dev, dev ^ hop) for dev in range(8)])
     blocks = gradient.reshape(local_rows, heads, HD)
     local_raw = jnp.einsum("rhi,rhj->hij", blocks, blocks, precision=lax.Precision.HIGHEST)
     gram_raw = lax.psum(local_raw, "node")

time: 207 us -> 201 us (0.971)
  waiting for transfers between devices: 166 us -> 153 us
  starting transfers between devices: 0.16 us -> 5.72 us
    ppermute x0 -> x3, waiting for transfers between devices: none -> 89.5 us  [per_device(): lax.ppermute(gradient, 'rep', [(dev, dev ^ hop) for dev in range(8)])]
    psum x1 -> x0, waiting for transfers between devices: 79.5 us -> none  [per_device(): gradient = lax.psum(partial_rows, 'rep')]
    all_gather x1, waiting for transfers between devices: 19.6 us -> 0.02 us  [per_device(): lax.all_gather(value_weight, 'node', axis=0, tiled=True)]
    ppermute x0 -> x3, starting transfers between devices: none -> 5.59 us  [per_device(): lax.ppermute(gradient, 'rep', [(dev, dev ^ hop) for dev in range(8)])]
    psum x1, waiting for transfers between devices: 31.8 us -> 29.1 us  [per_device(): gram_raw = lax.psum(local_raw, 'node')]
    reshape x1 -> x0, other arithmetic: 2.08 us -> none  [per_device(): blocks = gradient.reshape(local_rows, heads, HD)]
  transfers between devices with their start and end apart: 4 -> 6, of which waited for: 4 -> 5; matrix products, arithmetic and copies ran while one was open for 4% -> 4% of each run, Pallas kernels for 0% -> 0%
where the time goes in v2:
time: 201 us
  waiting for transfers between devices  153 us (76%)
  matrix products  20.4 us (10%)
  between operations  14 us (7%)
  starting transfers between devices  5.72 us (3%)
  other arithmetic  4.02 us (2%)
  local copies, waits for them, and re-layouts  3.72 us (2%)
    ppermute x3, waiting for transfers between devices, per_device(): lax.ppermute(gradient, 'rep', [(dev, dev ^ hop) for dev in range(8)])  89.5 us
    reduce_scatter x1, waiting for transfers between devices, per_device(): lax.psum_scatter(lax.dot_general(tokens, cotangent, (((0,), (0,)), ((), (...  34 us
    psum x1, waiting for transfers between devices, per_device(): gram_raw = lax.psum(local_raw, 'node')  29.1 us
    ppermute x3, starting transfers between devices, per_device(): lax.ppermute(gradient, 'rep', [(dev, dev ^ hop) for dev in range(8)])  5.59 us
  transfers between devices with their start and end apart: 6, of which 5 were waited for; matrix products, arithmetic and copies ran while one was open for 4% of the time, Pallas kernels for 0%

profile of v2, /device:TPU:0, one launch (start us, length us, event | category | flops | bytes accessed | tf_op | source)
XLA Modules:
  0.0 200.6 jit_solution(69287042591062721)
XLA Ops:
  7.2 0.0 copy-start
  7.2 0.0 reduce-scatter.2.cloned.1.call-start
  7.2 1.2 copy-done
  8.4 3.0 %convolution_convert_fusion = bf16[2048,512]{1,0:T(8,128)(2,1)} fusion(bf16[256,2048]{1,0:T(8,128)(2,1)S(1)} %copy-done, bf16[256,512]{1,0:T(8,128)(2,1)} %param.4), kind=kOutput, calls=%fused_computation | convolution fusion | flops 537919488 | bytes 3407872 | tf_op jit(solution)/shard_map/dot_general | solution.py:27
  11.4 0.0 reduce-scatter.2.cloned.1.call-update
  11.5 0.0 all-gather.2.cloned.1.call-start
  11.5 34.0 %reduce-scatter.2.cloned.1.call-done = bf16[512,512]{1,0:T(8,128)(2,1)} async-done(((bf16[2048,512]{1,0:T(8,128)(2,1)}), bf16[512,512]{1,0:T(8,128)(2,1)}) %reduce-scatter.2.cloned.1.call-update) | async-done | bytes 524304 | tf_op jit(solution)/shard_map/reduce_scatter | solution.py:26
  45.5 0.0 copy-start.1
  45.5 1.2 convert_element_type.15
  46.8 1.5 collective-permute-start
  48.3 0.0 all-gather.2.cloned.1.call-update
  48.3 0.0 all-reduce.2.cloned.1.call-start
  48.4 23.3 %collective-permute-done = f32[512,512]{1,0:T(8,128)} collective-permute-done((f32[512,512]{1,0:T(8,128)S(1)}, f32[512,512]{1,0:T(8,128)}, u32[]{:S(2)}, u32[]{:S(2)}) %collective-permute-start) | collective-permute-done | bytes 1048608 | tf_op jit(solution)/shard_map/ppermute | solution.py:36
  71.7 0.0 copy-done.1
  71.7 1.4 convert_add_fusion
  73.1 1.6 collective-permute-start.1
  74.6 22.4 %collective-permute-done.1 = f32[512,512]{1,0:T(8,128)S(1)} collective-permute-done((f32[512,512]{1,0:T(8,128)S(1)}, f32[512,512]{1,0:T(8,128)S(1)}, u32[]{:S(2)}, u32[]{:S(2)}) %collective-permute-start.1) | collective-permute-done | bytes 1048608 | tf_op jit(solution)/shard_map/ppermute | solution.py:36
  97.0 0.2 add.55
  97.2 0.0 copy-start.2
  97.2 2.5 %collective-permute-start.2 = (f32[512,512]{1,0:T(8,128)S(1)}, f32[512,512]{1,0:T(8,128)S(1)}, u32[]{:S(2)}, u32[]{:S(2)}) collective-permute-start(f32[512,512]{1,0:T(8,128)S(1)} %add.55), channel_id=1, source_target_pairs={{0,4},{1,5},{2,6},{3,7},{4,0},{5,1},{6,2},{7,3},{8,12},{9,13},{10,... | collective-permute-start | bytes 3145736 | tf_op jit(solution)/shard_map/ppermute | solution.py:36
  99.8 43.9 %collective-permute-done.2 = f32[512,512]{1,0:T(8,128)S(1)} collective-permute-done((f32[512,512]{1,0:T(8,128)S(1)}, f32[512,512]{1,0:T(8,128)S(1)}, u32[]{:S(2)}, u32[]{:S(2)}) %collective-permute-start.2) | collective-permute-done | bytes 1048608 | tf_op jit(solution)/shard_map/ppermute | solution.py:36
  143.6 2.7 %fusion.5 = f32[4,128,128]{2,1,0:T(8,128)} fusion(f32[512,512]{1,0:T(8,128)S(1)} %add.55, f32[512,512]{1,0:T(8,128)S(1)} %collective-permute-done.2), kind=kOutput, calls=%fused_computation.14 | convolution fusion | flops 402915328 | bytes 2359296 | tf_op jit(solution)/shard_map/rhi,rhj->hij/dot_general | solution.py:38
  146.3 0.0 all-reduce.2.cloned.1.call-update
  146.4 0.0 all-gather.2.cloned.1.call-done
  146.4 0.0 copy-done.2
  146.4 3.3 %convolution_convert_fusion.1 = bf16[256,2048]{1,0:T(8,128)(2,1)} fusion(bf16[256,512]{1,0:T(8,128)(2,1)S(1)} %copy-done.2, bf16[2048,512]{1,0:T(8,128)(2,1)} %all-gather.2.cloned.1.call-done), kind=kOutput, calls=%fused_computation.1 | convolution fusion | flops 537395200 | bytes 3407872 | tf_op jit(solution)/shard_map/dot_general | solution.py:20
  149.7 29.1 %all-reduce.2.cloned.1.call-done = f32[4,128,128]{2,1,0:T(8,128)} async-done(((f32[4,128,128]{2,1,0:T(8,128)}), f32[4,128,128]{2,1,0:T(8,128)}) %all-reduce.2.cloned.1.call-update) | async-done | bytes 262160 | tf_op jit(solution)/shard_map/psum | solution.py:39
  178.8 0.0 copy-start.3
  178.8 1.2 select_reduce_fusion
  180.0 1.6 fusion.4
  181.6 0.0 copy-done.3
  181.6 0.4 fusion.14
  182.0 0.6 fusion.16
  182.6 0.4 fusion.3
  183.0 0.4 fusion.18
  183.4 0.6 fusion.19
  184.0 0.4 fusion.2
  184.4 0.4 fusion.21
  184.8 0.6 fusion.22
  185.4 0.4 fusion.1
  185.8 0.4 fusion.24
  186.2 0.6 fusion.25
  186.8 0.4 fusion
  187.2 0.4 fusion.10
  187.6 0.4 fusion.17
  188.0 0.4 fusion.20
  188.4 0.4 fusion.23
  188.8 0.6 fusion.26
  189.4 2.1 %convolution_multiply_fusion = f32[4,128,512]{2,1,0:T(8,128)} fusion(f32[4,128,128]{1,2,0:T(8,128)S(1)} %fusion.26, f32[4]{0:T(128)S(1)} %get-tuple-element.4, f32[512,512]{1,0:T(8,128)S(1)} %add.55, f32[512,512]{1,0:T(8,128)S(1)} %collective-permute-done.2), kind=kOutput, calls=%fused_computation.2 | convolution fusion | flops 403439616 | bytes 3407888 | tf_op jit(solution)/shard_map/rhi,hij->rhj/dot_general | solution.py:56
  191.5 2.5 %copy.12 = f32[512,512]{1,0:T(8,128)} copy(f32[512,512]{0,1:T(8,128)} %bitcast.51) | data formatting | bytes 2097152
  (4 shorter events, 0.0 us)
Async XLA Ops:
  7.2 1.2 copy-start
  7.2 38.4 %reduce-scatter.2.cloned.1.call-start = ((), (), s32[]{:S(2)}) async-start(), calls=%async_computation.2 | async-start | bytes 2621440 | tf_op jit(solution)/shard_map/reduce_scatter | solution.py:26
  11.5 134.9 %all-gather.2.cloned.1.call-start = ((), (), s32[]{:S(2)}) async-start(), calls=%async_computation.1 | async-start | bytes 2621440 | tf_op jit(solution)/shard_map/all_gather | solution.py:22
  45.5 26.1 %copy-start.1 = (bf16[512,512]{1,0:T(8,128)(2,1)S(1)}, bf16[512,512]{1,0:T(8,128)(2,1)}, u32[]{:S(2)}) copy-start(bf16[512,512]{1,0:T(8,128)(2,1)} %reduce-scatter.2.cloned.1.call-done) | copy-start | bytes 1572868
  46.8 24.9 %collective-permute-start = (f32[512,512]{1,0:T(8,128)S(1)}, f32[512,512]{1,0:T(8,128)}, u32[]{:S(2)}, u32[]{:S(2)}) collective-permute-start(f32[512,512]{1,0:T(8,128)S(1)} %convert_element_type.15), channel_id=1, source_target_pairs={{0,1},{1,0},{2,3},{3,2},{4,5},{5,4},{6,7},{7,6},{8,9},{9,8},{10,11... | collective-permute-start | bytes 3145736 | tf_op jit(solution)/shard_map/ppermute | solution.py:36
  48.3 130.5 %all-reduce.2.cloned.1.call-start = ((), (), s32[]{:S(2)}) async-start(), calls=%async_computation.3 | async-start | bytes 524288 | tf_op jit(solution)/shard_map/psum | solution.py:39
  73.1 23.9 %collective-permute-start.1 = (f32[512,512]{1,0:T(8,128)S(1)}, f32[512,512]{1,0:T(8,128)S(1)}, u32[]{:S(2)}, u32[]{:S(2)}) collective-permute-start(f32[512,512]{1,0:T(8,128)S(1)} %convert_add_fusion), channel_id=1, source_target_pairs={{0,2},{1,3},{2,0},{3,1},{4,6},{5,7},{6,4},{7,5},{8,10},{9,11},{10,... | collective-permute-start | bytes 3145736 | tf_op jit(solution)/shard_map/ppermute | solution.py:36
  97.2 49.2 %copy-start.2 = (bf16[256,512]{1,0:T(8,128)(2,1)S(1)}, bf16[256,512]{1,0:T(8,128)(2,1)}, u32[]{:S(2)}) copy-start(bf16[256,512]{1,0:T(8,128)(2,1)} %param.4) | copy-start | bytes 786436
  97.2 46.4 %collective-permute-start.2 = (f32[512,512]{1,0:T(8,128)S(1)}, f32[512,512]{1,0:T(8,128)S(1)}, u32[]{:S(2)}, u32[]{:S(2)}) collective-permute-start(f32[512,512]{1,0:T(8,128)S(1)} %add.55), channel_id=1, source_target_pairs={{0,4},{1,5},{2,6},{3,7},{4,0},{5,1},{6,2},{7,3},{8,12},{9,13},{10,... | collective-permute-start | bytes 3145736 | tf_op jit(solution)/shard_map/ppermute | solution.py:36
  178.8 2.8 %copy-start.3 = (f32[4,128,128]{2,1,0:T(8,128)S(1)}, f32[4,128,128]{2,1,0:T(8,128)}, u32[]{:S(2)}) copy-start(f32[4,128,128]{2,1,0:T(8,128)} %all-reduce.2.cloned.1.call-done) | copy-start | bytes 786436
Sparse Core Ops, SparseCore 0:
  11.6 33.9 reduce-scatter.1
  48.4 21.6 all-gather.1
  146.5 32.2 all-reduce.1
